TPU v7x, 32 devices: a whole 2x2x4 slice. The times are simulated.
32 devices in a mesh: seq: 8 (over z, x), feat: 4 (over y, core).
Axes of the slice: x: 2, y: 2, z: 4, core: 2. Of those that a mesh axis runs over, the one named last changes fastest.
Arguments:
- injection: bfloat16 [1024, 5120], P('seq', 'feat'), may hold values from -8 to 8
- warm_start: bfloat16 [1024, 5120], P('seq', 'feat'), may hold values from -12 to 12
- gain_in: float32 [5120], replicated, may hold values from 0.5 to 1.5
- gain_out: float32 [5120], replicated, may hold values from 0.5 to 1.5
- w_query: bfloat16 [5120, 5120], P(None, 'feat'), may hold values from -0.0848993624 to 0.0848993624
- w_key: bfloat16 [5120, 1024], P(None, 'feat'), may hold values from -0.0848993624 to 0.0848993624
- w_value: bfloat16 [5120, 1024], P(None, 'feat'), may hold values from -0.078125 to 0.078125
- w_out: bfloat16 [5120, 5120], P('feat'), may hold values from -0.078125 to 0.078125
Outputs:
- equilibrium: float32 [1024, 5120], P('seq', 'feat')
All inputs are finite; a program needn't handle non-finite values.
Results may differ from a plain program's by a relative error of at most 0.009.
Values may be sent and summed in bfloat16 or wider, within the bound.
A program may use at most 128 MiB of HBM per device.

v0:
```python
import math
import jax
import jax.numpy as jnp
from jax import lax
from jax.sharding import PartitionSpec as P

HEADS = 40
KV_HEADS = 8
HEAD_DIM = 128
ITERS = 4
EPS = 1e-06
LAMBDA = 0.03


def solve_small(matrix, target):
    size_now = target.shape[0]
    row_list = [matrix[idx_row] for idx_row in range(size_now)]
    value_list = [target[idx_row] for idx_row in range(size_now)]
    for pivot_at in range(size_now):
        for below_at in range(pivot_at + 1, size_now):
            ratio_now = row_list[below_at][pivot_at] / row_list[pivot_at][pivot_at]
            row_list[below_at] = row_list[below_at] - ratio_now * row_list[pivot_at]
            value_list[below_at] = value_list[below_at] - ratio_now * value_list[pivot_at]
    result_list = [None] * size_now
    for pivot_at in reversed(range(size_now)):
        running = value_list[pivot_at]
        for later_at in range(pivot_at + 1, size_now):
            running = running - row_list[pivot_at][later_at] * result_list[later_at]
        result_list[pivot_at] = running / row_list[pivot_at][pivot_at]
    return jnp.stack(result_list)


def coefficients(gram_matrix, scale_all):
    history_len = gram_matrix.shape[0]
    system = gram_matrix / scale_all + LAMBDA * jnp.eye(history_len, dtype=jnp.float32)
    unscaled = solve_small(system, jnp.ones((history_len,), jnp.float32))
    return unscaled / jnp.sum(unscaled)


def on_device(injection, warm_start, gain_in, gain_out, w_query, w_key, w_value, w_out):
    seq_at = lax.axis_index("seq")
    tok_dev = injection.shape[0]
    width = gain_in.shape[0]
    head_cols = w_query.shape[1]
    kv_cols = w_key.shape[1]
    kv_local = kv_cols // HEAD_DIM
    group = HEADS // KV_HEADS
    scale_all = float(tok_dev * lax.axis_size("seq") * width)
    score_scale = 1.0 / math.sqrt(HEAD_DIM)
    w_joined = jnp.concatenate([w_query, w_key, w_value], axis=1)
    query_pos = seq_at * tok_dev + jnp.arange(tok_dev, dtype=jnp.int32)
    injection_here, start_here = (
        lax.all_to_all(injection, "feat", split_axis=0, concat_axis=1, tiled=True),
        lax.all_to_all(warm_start, "feat", split_axis=0, concat_axis=1, tiled=True),
    )
    injection_full = injection_here.astype(jnp.float32)
    current = start_here.astype(jnp.float32)
    evaluated = []
    residuals = []
    for iteration in range(ITERS):
        mixed = current + injection_full
        normed = (
            mixed * lax.rsqrt(jnp.mean(mixed * mixed, axis=1, keepdims=True) + EPS) * gain_in
        ).astype(jnp.bfloat16)
        layer_joined = jnp.dot(
            lax.all_gather(normed, "feat", axis=0, tiled=True),
            w_joined,
            preferred_element_type=jnp.float32,
        ).astype(jnp.bfloat16)
        queries = layer_joined[:, :head_cols].reshape(tok_dev, kv_local, group, HEAD_DIM)
        key_rows = layer_joined[:, head_cols : head_cols + kv_cols]
        value_rows = layer_joined[:, head_cols + kv_cols :]
        start_max = jnp.full((tok_dev, kv_local, group), -1e30, jnp.float32)
        run_max = start_max
        key_piece = lax.all_gather(key_rows, "seq", axis=0, tiled=True)
        value_piece = lax.all_gather(value_rows, "seq", axis=0, tiled=True)
        length = key_piece.shape[0]
        key_heads = key_piece.reshape(length, kv_local, HEAD_DIM)
        value_heads = value_piece.reshape(length, kv_local, HEAD_DIM)
        scores = (
            jnp.einsum("tkgd,skd->tkgs", queries, key_heads, preferred_element_type=jnp.float32)
            * score_scale
        )
        key_pos = jnp.arange(length, dtype=jnp.int32)
        allowed = (query_pos[:, None] >= key_pos[None, :])[:, None, None, :]
        scores = jnp.where(allowed, scores, -1e30)
        new_max = jnp.maximum(run_max, jnp.max(scores, axis=3))
        weights = jnp.where(allowed, jnp.exp(scores - new_max[..., None]), 0.0)
        run_sum = jnp.sum(weights, axis=3)
        run_acc = jnp.einsum(
            "tkgs,skd->tkgd",
            weights.astype(jnp.bfloat16),
            value_heads,
            preferred_element_type=jnp.float32,
        )
        run_max, run_sum, run_acc = (new_max, run_sum, run_acc)
        attended = (run_acc / run_sum[..., None]).astype(jnp.bfloat16).reshape(tok_dev, head_cols)
        update = lax.psum_scatter(
            jnp.dot(attended, w_out, preferred_element_type=jnp.float32),
            "feat",
            scatter_dimension=0,
            tiled=True,
        )
        summed = mixed + update
        image = (
            summed * lax.rsqrt(jnp.mean(summed * summed, axis=1, keepdims=True) + EPS) * gain_out
        )
        evaluated.append(image)
        residuals.append(image - current)
        if iteration == 0:
            current = image
        else:
            history_len = iteration + 1
            stacked = jnp.stack(residuals).reshape(history_len, -1)
            local_gram = jnp.dot(stacked, stacked.T, precision=lax.Precision.HIGHEST)
            gram_matrix = lax.psum(local_gram, ("seq", "feat"))
            weights_now = coefficients(gram_matrix, scale_all)
            current = weights_now[0] * evaluated[0]
            for other in range(1, history_len):
                current = current + weights_now[other] * evaluated[other]
    return lax.all_to_all(current, "feat", split_axis=1, concat_axis=0, tiled=True)


def solution(mesh):
    in_specs = (
        P("seq", "feat"),
        P("seq", "feat"),
        P(),
        P(),
        P(None, "feat"),
        P(None, "feat"),
        P(None, "feat"),
        P("feat", None),
    )
    out_specs = P("seq", "feat")
    return jax.shard_map(
        on_device, mesh=mesh, in_specs=in_specs, out_specs=out_specs, check_vma=False
    )
```

profile of v0, /device:TPU:0, one launch (start us, length us, event | category | flops | bytes accessed | tf_op | source)
XLA Modules:
  0.0 838.7 jit_solution(10279321022507677067)
XLA Ops:
  6.5 11.1 %all_to_all.45 = bf16[4,32,1280]{2,1,0:T(8,128)(2,1)S(1)} all-to-all(bf16[4,32,1280]{2,1,0:T(8,128)(2,1)} %bitcast.259), channel_id=1, replica_groups=mesh['seq'=8,'feat'=4] {'feat'}, dimensions={0} | all-to-all | bytes 655360 | tf_op jit(solution)/shard_map/all_to_all | solution.py:53
  29.1 10.9 %constant_dynamic-update-slice_fusion.2 = bf16[5120,1792]{1,0:T(8,128)(2,1)} fusion(bf16[5120,1280]{1,0:T(8,128)(2,1)} %param.12), kind=kLoop, calls=%fused_computation.95 | loop fusion | bytes 26214400
  58.2 31.4 %all_gather.37 = bf16[1024,256]{1,0:T(8,128)(2,1)S(1)} all-gather(bf16[128,256]{1,0:T(8,128)(2,1)S(1)} %get-tuple-element.30), channel_id=1, replica_groups=mesh['seq'=8,'feat'=4] {'seq'}, dimensions={0}, use_global_device_ids=true | all-gather | bytes 589824 | tf_op jit(solution)/shard_map/all_gather | solution.py:76
  92.6 33.4 %all_gather.38 = bf16[1024,256]{1,0:T(8,128)(2,1)} all-gather(bf16[128,256]{1,0:T(8,128)(2,1)S(1)} %get-tuple-element.29), channel_id=1, replica_groups=mesh['seq'=8,'feat'=4] {'seq'}, dimensions={0}, use_global_device_ids=true | all-gather | bytes 589824 | tf_op jit(solution)/shard_map/all_gather | solution.py:75
  136.5 34.7 %reduce-scatter.5.cloned.1.call-done = f32[32,5120]{1,0:T(8,128)} async-done(((f32[128,5120]{1,0:T(8,128)}), f32[32,5120]{1,0:T(8,128)}) %reduce-scatter.5.cloned.1.call-update) | async-done | bytes 655376 | tf_op jit(solution)/shard_map/reduce_scatter | solution.py:98
  174.9 18.0 %all-gather.7.cloned.1.call-done = bf16[128,5120]{1,0:T(8,128)(2,1)} async-done(((bf16[32,5120]{1,0:T(8,128)(2,1)}), bf16[128,5120]{1,0:T(8,128)(2,1)}) %all-gather.7.cloned.1.call-update) | async-done | bytes 1310736 | tf_op jit(solution)/shard_map/all_gather | solution.py:66
  202.8 31.4 %all_gather.40 = bf16[1024,256]{1,0:T(8,128)(2,1)S(1)} all-gather(bf16[128,256]{1,0:T(8,128)(2,1)S(1)} %get-tuple-element.28), channel_id=1, replica_groups=mesh['seq'=8,'feat'=4] {'seq'}, dimensions={0}, use_global_device_ids=true | all-gather | bytes 589824 | tf_op jit(solution)/shard_map/all_gather | solution.py:76
  237.2 33.4 %all_gather.41 = bf16[1024,256]{1,0:T(8,128)(2,1)} all-gather(bf16[128,256]{1,0:T(8,128)(2,1)S(1)} %get-tuple-element.27), channel_id=1, replica_groups=mesh['seq'=8,'feat'=4] {'seq'}, dimensions={0}, use_global_device_ids=true | all-gather | bytes 589824 | tf_op jit(solution)/shard_map/all_gather | solution.py:75
  281.5 34.2 %reduce-scatter.7.cloned.1.call-done = f32[32,5120]{1,0:T(8,128)} async-done(((f32[128,5120]{1,0:T(8,128)}), f32[32,5120]{1,0:T(8,128)}) %reduce-scatter.7.cloned.1.call-update) | async-done | bytes 655376 | tf_op jit(solution)/shard_map/reduce_scatter | solution.py:98
  319.5 12.0 %fusion.48 = f32[2,2]{1,0:T(2,128)S(1)} fusion(f32[2,32,5120]{2,1,0:T(8,128)S(1)} %pad_maximum_fusion.2), kind=kOutput, calls=%fused_computation.47 | convolution fusion | flops 7864320 | bytes 1310736 | tf_op jit(solution)/shard_map/dot_general | solution.py:115
  331.5 39.2 %psum.21 = f32[2,2]{1,0:T(2,128)S(1)} all-reduce(f32[2,2]{1,0:T(2,128)S(1)} %fusion.48), channel_id=1, replica_groups=mesh['seq'=8,'feat'=4] {'seq','feat'}, use_global_device_ids=true, to_apply=%region_10.11 | all-reduce | flops 4 | bytes 32 | tf_op jit(solution)/shard_map/psum | solution.py:116
  379.4 18.8 %all-gather.9.cloned.1.call-done = bf16[128,5120]{1,0:T(8,128)(2,1)} async-done(((bf16[32,5120]{1,0:T(8,128)(2,1)}), bf16[128,5120]{1,0:T(8,128)(2,1)}) %all-gather.9.cloned.1.call-update) | async-done | bytes 1310736 | tf_op jit(solution)/shard_map/all_gather | solution.py:66
  408.8 31.5 %all_gather.43 = bf16[1024,256]{1,0:T(8,128)(2,1)S(1)} all-gather(bf16[128,256]{1,0:T(8,128)(2,1)S(1)} %get-tuple-element.26), channel_id=1, replica_groups=mesh['seq'=8,'feat'=4] {'seq'}, dimensions={0}, use_global_device_ids=true | all-gather | bytes 589824 | tf_op jit(solution)/shard_map/all_gather | solution.py:76
  442.4 33.7 %all_gather.44 = bf16[1024,256]{1,0:T(8,128)(2,1)} all-gather(bf16[128,256]{1,0:T(8,128)(2,1)} %get-tuple-element.25), channel_id=1, replica_groups=mesh['seq'=8,'feat'=4] {'seq'}, dimensions={0}, use_global_device_ids=true | all-gather | bytes 589824 | tf_op jit(solution)/shard_map/all_gather | solution.py:75
  485.9 34.5 %reduce-scatter.9.cloned.1.call-done = f32[32,5120]{1,0:T(8,128)} async-done(((f32[128,5120]{1,0:T(8,128)}), f32[32,5120]{1,0:T(8,128)}) %reduce-scatter.9.cloned.1.call-update) | async-done | bytes 655376 | tf_op jit(solution)/shard_map/reduce_scatter | solution.py:98
  525.7 13.0 %fusion.42 = f32[3,3]{1,0:T(4,128)S(1)} fusion(f32[3,32,5120]{2,1,0:T(8,128)S(1)} %pad_maximum_fusion.1), kind=kOutput, calls=%fused_computation.45 | convolution fusion | flops 17694720 | bytes 1966116 | tf_op jit(solution)/shard_map/dot_general | solution.py:115
  538.7 39.2 %psum.22 = f32[3,3]{1,0:T(4,128)S(1)} all-reduce(f32[3,3]{1,0:T(4,128)S(1)} %fusion.42), channel_id=1, replica_groups=mesh['seq'=8,'feat'=4] {'seq','feat'}, use_global_device_ids=true, to_apply=%region_16.17 | all-reduce | flops 9 | bytes 72 | tf_op jit(solution)/shard_map/psum | solution.py:116
  593.7 19.0 %all-gather.11.cloned.1.call-done = bf16[128,5120]{1,0:T(8,128)(2,1)} async-done(((bf16[32,5120]{1,0:T(8,128)(2,1)}), bf16[128,5120]{1,0:T(8,128)(2,1)}) %all-gather.11.cloned.1.call-update) | async-done | bytes 1310736 | tf_op jit(solution)/shard_map/all_gather | solution.py:66
  622.7 31.6 %all_gather.46 = bf16[1024,256]{1,0:T(8,128)(2,1)S(1)} all-gather(bf16[128,256]{1,0:T(8,128)(2,1)S(1)} %get-tuple-element.24), channel_id=1, replica_groups=mesh['seq'=8,'feat'=4] {'seq'}, dimensions={0}, use_global_device_ids=true | all-gather | bytes 589824 | tf_op jit(solution)/shard_map/all_gather | solution.py:76
  657.2 33.8 %all_gather.47 = bf16[1024,256]{1,0:T(8,128)(2,1)} all-gather(bf16[128,256]{1,0:T(8,128)(2,1)S(1)} %get-tuple-element.23), channel_id=1, replica_groups=mesh['seq'=8,'feat'=4] {'seq'}, dimensions={0}, use_global_device_ids=true | all-gather | bytes 589824 | tf_op jit(solution)/shard_map/all_gather | solution.py:75
  701.4 34.8 %reduce-scatter.11.cloned.1.call-done = f32[32,5120]{1,0:T(8,128)} async-done(((f32[128,5120]{1,0:T(8,128)}), f32[32,5120]{1,0:T(8,128)}) %reduce-scatter.11.cloned.1.call-update) | async-done | bytes 655376 | tf_op jit(solution)/shard_map/reduce_scatter | solution.py:98
  741.2 13.6 %fusion.45 = f32[4,4]{1,0:T(4,128)S(1)} fusion(f32[4,32,5120]{2,1,0:T(8,128)S(1)} %pad_maximum_fusion), kind=kOutput, calls=%fused_computation.46 | convolution fusion | flops 31457280 | bytes 2621504 | tf_op jit(solution)/shard_map/dot_general | solution.py:115
  754.9 39.2 %psum.23 = f32[4,4]{1,0:T(4,128)S(1)} all-reduce(f32[4,4]{1,0:T(4,128)S(1)} %fusion.45), channel_id=1, replica_groups=mesh['seq'=8,'feat'=4] {'seq','feat'}, use_global_device_ids=true, to_apply=%region_22.23 | all-reduce | flops 16 | bytes 128 | tf_op jit(solution)/shard_map/psum | solution.py:116
  817.3 13.6 %all_to_all.46 = f32[32,4,1280]{2,0,1:T(8,128)S(1)} all-to-all(f32[32,4,1280]{2,0,1:T(8,128)S(1)} %bitcast.240), channel_id=1, replica_groups=mesh['seq'=8,'feat'=4] {'feat'}, dimensions={1} | all-to-all | bytes 1310720 | tf_op jit(solution)/shard_map/all_to_all | solution.py:121
  (192 shorter events, 153.5 us)
Async XLA Ops:
  6.5 21.6 %copy-start.13 = (f32[5120]{0:T(1024)S(1)}, f32[5120]{0:T(1024)}, u32[]{:S(2)}) copy-start(f32[5120]{0:T(1024)} %param.10) | copy-start | bytes 61444
  17.6 10.1 %all-to-all-start = ((bf16[4,32,1280]{2,1,0:T(8,128)(2,1)}), bf16[4,32,1280]{2,1,0:T(8,128)(2,1)S(1)}, u32[]{:S(2)}, u32[]{:S(2)}) async-start(bf16[4,32,1280]{2,1,0:T(8,128)(2,1)} %bitcast.260), calls=%async_computation | async-start | bytes 655360 | tf_op jit(solution)/shard_map/all_to_all | solution.py:54
  21.1 27.2 %all-gather.5.cloned.1.call-start = ((), (), s32[]{:S(2)}) async-start(), calls=%async_computation.7 | async-start | bytes 1638400 | tf_op jit(solution)/shard_map/all_gather | solution.py:66
  29.0 142.2 %reduce-scatter.5.cloned.1.call-start = ((), (), s32[]{:S(2)}) async-start(), calls=%async_computation.8 | async-start | bytes 3276800 | tf_op jit(solution)/shard_map/reduce_scatter | solution.py:98
  39.9 3.7 copy-start.7
  90.7 41.4 %slice-start = ((s8[13107200]{0:T(1024)(128)(4,1)}), s8[524288]{0:T(1024)(128)(4,1)S(1)}, s32[]{:S(2)}) async-start(s8[13107200]{0:T(1024)(128)(4,1)} %bitcast.226), calls=%async_computation.15 | async-start | bytes 1048576
  127.2 3.4 copy-start.10
  127.2 4.8 slice-start.1
  133.0 39.5 %copy-start.8 = (f32[5120]{0:T(1024)S(1)}, f32[5120]{0:T(1024)}, u32[]{:S(2)}) copy-start(f32[5120]{0:T(1024)} %param.11) | copy-start | bytes 61444
  136.4 56.4 %all-gather.7.cloned.1.call-start = ((), (), s32[]{:S(2)}) async-start(), calls=%async_computation.9 | async-start | bytes 1638400 | tf_op jit(solution)/shard_map/all_gather | solution.py:66
  172.8 145.5 %copy-start = (f32[1,32,5120]{2,1,0:T(8,128)}, f32[1,32,5120]{2,1,0:T(8,128)S(1)}, u32[]{:S(2)}) copy-start(f32[1,32,5120]{2,1,0:T(8,128)S(1)} %get-tuple-element.22) | copy-start | bytes 1966084
  174.5 141.2 %reduce-scatter.7.cloned.1.call-start = ((), (), s32[]{:S(2)}) async-start(), calls=%async_computation.10 | async-start | bytes 3276800 | tf_op jit(solution)/shard_map/reduce_scatter | solution.py:98
  235.2 41.4 %slice-start.4 = ((s8[13107200]{0:T(1024)(128)(4,1)}), s8[524288]{0:T(1024)(128)(4,1)S(1)}, s32[]{:S(2)}) async-start(s8[13107200]{0:T(1024)(128)(4,1)} %bitcast.228), calls=%async_computation.19 | async-start | bytes 1048576
  271.8 3.4 copy-start.11
  271.8 4.8 slice-start.5
  281.0 117.3 %all-gather.9.cloned.1.call-start = ((), (), s32[]{:S(2)}) async-start(), calls=%async_computation.11 | async-start | bytes 1638400 | tf_op jit(solution)/shard_map/all_gather | solution.py:66
  379.2 141.3 %reduce-scatter.9.cloned.1.call-start = ((), (), s32[]{:S(2)}) async-start(), calls=%async_computation.12 | async-start | bytes 3276800 | tf_op jit(solution)/shard_map/reduce_scatter | solution.py:98
  440.2 40.7 %slice-start.8 = ((s8[13107200]{0:T(1024)(128)(4,1)}), s8[524288]{0:T(1024)(128)(4,1)S(1)}, s32[]{:S(2)}) async-start(s8[13107200]{0:T(1024)(128)(4,1)} %bitcast.230), calls=%async_computation.23 | async-start | bytes 1048576
  477.3 3.7 slice-start.9
  485.6 127.1 %all-gather.11.cloned.1.call-start = ((), (), s32[]{:S(2)}) async-start(), calls=%async_computation.13 | async-start | bytes 1638400 | tf_op jit(solution)/shard_map/all_gather | solution.py:66
  593.7 142.5 %reduce-scatter.11.cloned.1.call-start = ((), (), s32[]{:S(2)}) async-start(), calls=%async_computation.14 | async-start | bytes 3276800 | tf_op jit(solution)/shard_map/reduce_scatter | solution.py:98
  622.7 74.3 %slice-start.12 = ((s8[13107200]{0:T(1024)(128)(4,1)}), s8[524288]{0:T(1024)(128)(4,1)S(1)}, s32[]{:S(2)}) async-start(s8[13107200]{0:T(1024)(128)(4,1)} %bitcast.232), calls=%async_computation.27 | async-start | bytes 1048576
  692.1 4.8 slice-start.13
  701.4 38.4 %copy-start.1 = (f32[1,32,5120]{2,1,0:T(8,128)S(1)}, f32[1,32,5120]{2,1,0:T(8,128)}, u32[]{:S(2)}) copy-start(f32[1,32,5120]{2,1,0:T(8,128)} %copy-done) | copy-start | bytes 1966084
  (15 other events, 31.1 us)
Sparse Core Ops, SparseCore 0:
  29.1 19.0 all-gather.4
  136.5 34.6 reduce-scatter.4
  174.7 18.1 all-gather.6
  281.1 34.6 reduce-scatter.6
  379.3 18.8 all-gather.8
  485.8 34.6 reduce-scatter.8
  593.8 18.8 all-gather.10
  701.5 34.6 reduce-scatter.10
where the time goes:
time: 848 us; the launch traced here: 839 us
  blocking collectives  403 us (48%)
  waiting for transfers between devices  204 us (24%)
  matrix products  102 us (12%)
  local copies, waits for them, and re-layouts  54.8 us (6%)
  between operations  39 us (5%)
  other arithmetic  31.9 us (4%)
    reduce_scatter x4, waiting for transfers between devices, on_device(): lax.psum_scatter(jnp.dot(attended, w_out, preferred_element_type=jnp.floa...  138 us
    all_gather x4, blocking collectives, on_device(): key_piece = lax.all_gather(key_rows, 'seq', axis=0, tiled=True)  134 us
    all_gather x4, blocking collectives, on_device(): value_piece = lax.all_gather(value_rows, 'seq', axis=0, tiled=True)  126 us
    psum x3, blocking collectives, on_device(): gram_matrix = lax.psum(local_gram, ('seq', 'feat'))  118 us
    all_gather x4, waiting for transfers between devices, on_device(): lax.all_gather(normed, 'feat', axis=0, tiled=True)  58.7 us
    dot_general x3, matrix products, on_device(): local_gram = jnp.dot(stacked, stacked.T, precision=lax.Precision.HIGHEST)  38.6 us
    dot_general x4, matrix products, on_device(): jnp.dot(lax.all_gather(normed, 'feat', axis=0, tiled=True), w_joined, pre...  36.7 us
    unnamed x63, local copies, waits for them, and re-layouts  23.7 us
  transfers between devices with their start and end apart: 9, of which 9 were waited for; matrix products, arithmetic and copies ran while one was open for 2% of the time, Pallas kernels for 0%

commit v1 on v0

--- a/solution.py
+++ b/solution.py
@@ -72,8 +72,13 @@
         value_rows = layer_joined[:, head_cols + kv_cols :]
         start_max = jnp.full((tok_dev, kv_local, group), -1e30, jnp.float32)
         run_max = start_max
-        key_piece = lax.all_gather(key_rows, "seq", axis=0, tiled=True)
-        value_piece = lax.all_gather(value_rows, "seq", axis=0, tiled=True)
+        key_piece, value_piece = jnp.split(
+            lax.all_gather(
+                jnp.concatenate([key_rows, value_rows], axis=1), "seq", axis=0, tiled=True
+            ),
+            [key_rows.shape[1]],
+            axis=1,
+        )
         length = key_piece.shape[0]
         key_heads = key_piece.reshape(length, kv_local, HEAD_DIM)
         value_heads = value_piece.reshape(length, kv_local, HEAD_DIM)

time: 848 us -> 745 us (0.88)
  blocking collectives: 403 us -> 142 us
  waiting for transfers between devices: 204 us -> 357 us
    all_gather x8 -> x0, blocking collectives: 260 us -> none  [the longest x4 134 us: on_device(): key_piece = lax.all_gather(key_rows, 'seq', axis=0, tiled=True)]
    all_gather x0 -> x4, waiting for transfers between devices: none -> 158 us  [on_device(): lax.all_gather(jnp.concatenate([key_rows, value_rows], axis=1), 'seq', ax...]
  transfers between devices with their start and end apart: 9 -> 13, of which waited for: 9 -> 13; matrix products, arithmetic and copies ran while one was open for 2% -> 2% of each run, Pallas kernels for 0% -> 0%
where the time goes in v1:
time: 745 us; the launch traced here: 736 us
  waiting for transfers between devices  357 us (48%)
  blocking collectives  142 us (19%)
  matrix products  102 us (14%)
  local copies, waits for them, and re-layouts  56.8 us (8%)
  between operations  39.3 us (5%)
  other arithmetic  33 us (4%)
    all_gather x4, waiting for transfers between devices, on_device(): lax.all_gather(jnp.concatenate([key_rows, value_rows], axis=1), 'seq', ax...  158 us
    reduce_scatter x4, waiting for transfers between devices, on_device(): lax.psum_scatter(jnp.dot(attended, w_out, preferred_element_type=jnp.floa...  133 us
    psum x3, blocking collectives, on_device(): gram_matrix = lax.psum(local_gram, ('seq', 'feat'))  118 us
    all_gather x4, waiting for transfers between devices, on_device(): lax.all_gather(normed, 'feat', axis=0, tiled=True)  59.6 us
    dot_general x3, matrix products, on_device(): local_gram = jnp.dot(stacked, stacked.T, precision=lax.Precision.HIGHEST)  38.6 us
    dot_general x4, matrix products, on_device(): jnp.dot(lax.all_gather(normed, 'feat', axis=0, tiled=True), w_joined, pre...  36.7 us
    unnamed x63, local copies, waits for them, and re-layouts  22.1 us
  transfers between devices with their start and end apart: 13, of which 13 were waited for; matrix products, arithmetic and copies ran while one was open for 2% of the time, Pallas kernels for 0%

profile of v1, /device:TPU:0, one launch (start us, length us, event | category | flops | bytes accessed | tf_op | source)
XLA Modules:
  0.0 735.7 jit_solution(2707644298306511193)
XLA Ops:
  6.5 11.1 %all_to_all.45 = bf16[4,32,1280]{2,1,0:T(8,128)(2,1)S(1)} all-to-all(bf16[4,32,1280]{2,1,0:T(8,128)(2,1)} %bitcast.259), channel_id=1, replica_groups=mesh['seq'=8,'feat'=4] {'feat'}, dimensions={0} | all-to-all | bytes 655360 | tf_op jit(solution)/shard_map/all_to_all | solution.py:53
  29.1 11.1 %constant_dynamic-update-slice_fusion.2 = bf16[5120,1792]{1,0:T(8,128)(2,1)} fusion(bf16[5120,1280]{1,0:T(8,128)(2,1)} %param.12), kind=kLoop, calls=%fused_computation.95 | loop fusion | bytes 26214400
  48.3 9.2 %convolution_convert_fusion.3 = bf16[128,1792]{1,0:T(8,128)(2,1)S(1)} fusion(bf16[128,5120]{1,0:T(8,128)(2,1)} %all-gather.9.cloned.1.call-done, bf16[5120,1792]{1,0:T(8,128)(2,1)} %constant_dynamic-update-slice_fusion), kind=kOutput, calls=%fused_computation.36 | convolution fusion | flops 2349039616 | bytes 20119552 | tf_op jit(solution)/shard_map/dot_general | solution.py:65
  59.2 39.3 %all-gather.11.cloned.1.call-done = bf16[1024,512]{1,0:T(8,128)(2,1)} async-done(((bf16[128,512]{1,0:T(8,128)(2,1)}), bf16[1024,512]{1,0:T(8,128)(2,1)}) %all-gather.11.cloned.1.call-update) | async-done | bytes 1048592 | tf_op jit(solution)/shard_map/all_gather | solution.py:76
  112.1 33.3 %reduce-scatter.5.cloned.1.call-done = f32[32,5120]{1,0:T(8,128)} async-done(((f32[128,5120]{1,0:T(8,128)}), f32[32,5120]{1,0:T(8,128)}) %reduce-scatter.5.cloned.1.call-update) | async-done | bytes 655376 | tf_op jit(solution)/shard_map/reduce_scatter | solution.py:103
  149.1 18.0 %all-gather.13.cloned.1.call-done = bf16[128,5120]{1,0:T(8,128)(2,1)} async-done(((bf16[32,5120]{1,0:T(8,128)(2,1)}), bf16[128,5120]{1,0:T(8,128)(2,1)}) %all-gather.13.cloned.1.call-update) | async-done | bytes 1310736 | tf_op jit(solution)/shard_map/all_gather | solution.py:66
  167.0 9.2 %convolution_convert_fusion.2 = bf16[128,1792]{1,0:T(8,128)(2,1)S(1)} fusion(bf16[128,5120]{1,0:T(8,128)(2,1)} %all-gather.13.cloned.1.call-done, bf16[5120,1792]{1,0:T(8,128)(2,1)} %constant_dynamic-update-slice_fusion), kind=kOutput, calls=%fused_computation.35 | convolution fusion | flops 2349039616 | bytes 20119552 | tf_op jit(solution)/shard_map/dot_general | solution.py:65
  177.9 39.4 %all-gather.15.cloned.1.call-done = bf16[1024,512]{1,0:T(8,128)(2,1)} async-done(((bf16[128,512]{1,0:T(8,128)(2,1)}), bf16[1024,512]{1,0:T(8,128)(2,1)}) %all-gather.15.cloned.1.call-update) | async-done | bytes 1048592 | tf_op jit(solution)/shard_map/all_gather | solution.py:76
  231.4 32.8 %reduce-scatter.7.cloned.1.call-done = f32[32,5120]{1,0:T(8,128)} async-done(((f32[128,5120]{1,0:T(8,128)}), f32[32,5120]{1,0:T(8,128)}) %reduce-scatter.7.cloned.1.call-update) | async-done | bytes 655376 | tf_op jit(solution)/shard_map/reduce_scatter | solution.py:103
  267.9 12.0 %fusion.48 = f32[2,2]{1,0:T(2,128)S(1)} fusion(f32[2,32,5120]{2,1,0:T(8,128)S(1)} %pad_maximum_fusion.2), kind=kOutput, calls=%fused_computation.47 | convolution fusion | flops 7864320 | bytes 1310736 | tf_op jit(solution)/shard_map/dot_general | solution.py:120
  279.9 39.2 %psum.21 = f32[2,2]{1,0:T(2,128)S(1)} all-reduce(f32[2,2]{1,0:T(2,128)S(1)} %fusion.48), channel_id=1, replica_groups=mesh['seq'=8,'feat'=4] {'seq','feat'}, use_global_device_ids=true, to_apply=%region_10.11 | all-reduce | flops 4 | bytes 32 | tf_op jit(solution)/shard_map/psum | solution.py:121
  327.7 18.9 %all-gather.17.cloned.1.call-done = bf16[128,5120]{1,0:T(8,128)(2,1)} async-done(((bf16[32,5120]{1,0:T(8,128)(2,1)}), bf16[128,5120]{1,0:T(8,128)(2,1)}) %all-gather.17.cloned.1.call-update) | async-done | bytes 1310736 | tf_op jit(solution)/shard_map/all_gather | solution.py:66
  346.6 9.2 %convolution_convert_fusion.1 = bf16[128,1792]{1,0:T(8,128)(2,1)S(1)} fusion(bf16[128,5120]{1,0:T(8,128)(2,1)} %all-gather.17.cloned.1.call-done, bf16[5120,1792]{1,0:T(8,128)(2,1)} %constant_dynamic-update-slice_fusion), kind=kOutput, calls=%fused_computation.34 | convolution fusion | flops 2349039616 | bytes 20119552 | tf_op jit(solution)/shard_map/dot_general | solution.py:65
  356.8 40.1 %all-gather.19.cloned.1.call-done = bf16[1024,512]{1,0:T(8,128)(2,1)} async-done(((bf16[128,512]{1,0:T(8,128)(2,1)}), bf16[1024,512]{1,0:T(8,128)(2,1)}) %all-gather.19.cloned.1.call-update) | async-done | bytes 1048592 | tf_op jit(solution)/shard_map/all_gather | solution.py:76
  409.9 33.1 %reduce-scatter.9.cloned.1.call-done = f32[32,5120]{1,0:T(8,128)} async-done(((f32[128,5120]{1,0:T(8,128)}), f32[32,5120]{1,0:T(8,128)}) %reduce-scatter.9.cloned.1.call-update) | async-done | bytes 655376 | tf_op jit(solution)/shard_map/reduce_scatter | solution.py:103
  448.2 13.0 %fusion.42 = f32[3,3]{1,0:T(4,128)S(1)} fusion(f32[3,32,5120]{2,1,0:T(8,128)S(1)} %pad_maximum_fusion.1), kind=kOutput, calls=%fused_computation.45 | convolution fusion | flops 17694720 | bytes 1966116 | tf_op jit(solution)/shard_map/dot_general | solution.py:120
  461.2 39.3 %psum.22 = f32[3,3]{1,0:T(4,128)S(1)} all-reduce(f32[3,3]{1,0:T(4,128)S(1)} %fusion.42), channel_id=1, replica_groups=mesh['seq'=8,'feat'=4] {'seq','feat'}, use_global_device_ids=true, to_apply=%region_16.17 | all-reduce | flops 9 | bytes 72 | tf_op jit(solution)/shard_map/psum | solution.py:121
  517.0 19.0 %all-gather.21.cloned.1.call-done = bf16[128,5120]{1,0:T(8,128)(2,1)} async-done(((bf16[32,5120]{1,0:T(8,128)(2,1)}), bf16[128,5120]{1,0:T(8,128)(2,1)}) %all-gather.21.cloned.1.call-update) | async-done | bytes 1310736 | tf_op jit(solution)/shard_map/all_gather | solution.py:66
  536.1 9.2 %convolution_convert_fusion = bf16[128,1792]{1,0:T(8,128)(2,1)S(1)} fusion(bf16[128,5120]{1,0:T(8,128)(2,1)} %all-gather.21.cloned.1.call-done, bf16[5120,1792]{1,0:T(8,128)(2,1)} %constant_dynamic-update-slice_fusion), kind=kOutput, calls=%fused_computation.33 | convolution fusion | flops 2349039616 | bytes 20119552 | tf_op jit(solution)/shard_map/dot_general | solution.py:65
  547.3 39.0 %all-gather.23.cloned.1.call-done = bf16[1024,512]{1,0:T(8,128)(2,1)} async-done(((bf16[128,512]{1,0:T(8,128)(2,1)}), bf16[1024,512]{1,0:T(8,128)(2,1)}) %all-gather.23.cloned.1.call-update) | async-done | bytes 1048592 | tf_op jit(solution)/shard_map/all_gather | solution.py:76
  599.8 33.4 %reduce-scatter.11.cloned.1.call-done = f32[32,5120]{1,0:T(8,128)} async-done(((f32[128,5120]{1,0:T(8,128)}), f32[32,5120]{1,0:T(8,128)}) %reduce-scatter.11.cloned.1.call-update) | async-done | bytes 655376 | tf_op jit(solution)/shard_map/reduce_scatter | solution.py:103
  638.3 13.6 %fusion.45 = f32[4,4]{1,0:T(4,128)S(1)} fusion(f32[4,32,5120]{2,1,0:T(8,128)S(1)} %pad_maximum_fusion), kind=kOutput, calls=%fused_computation.46 | convolution fusion | flops 31457280 | bytes 2621504 | tf_op jit(solution)/shard_map/dot_general | solution.py:120
  651.9 39.2 %psum.23 = f32[4,4]{1,0:T(4,128)S(1)} all-reduce(f32[4,4]{1,0:T(4,128)S(1)} %fusion.45), channel_id=1, replica_groups=mesh['seq'=8,'feat'=4] {'seq','feat'}, use_global_device_ids=true, to_apply=%region_22.23 | all-reduce | flops 16 | bytes 128 | tf_op jit(solution)/shard_map/psum | solution.py:121
  714.2 13.6 %all_to_all.46 = f32[32,4,1280]{2,0,1:T(8,128)S(1)} all-to-all(f32[32,4,1280]{2,0,1:T(8,128)S(1)} %bitcast.240), channel_id=1, replica_groups=mesh['seq'=8,'feat'=4] {'feat'}, dimensions={1} | all-to-all | bytes 1310720 | tf_op jit(solution)/shard_map/all_to_all | solution.py:126
  (200 shorter events, 121.1 us)
Async XLA Ops:
  6.5 21.6 %copy-start.13 = (f32[5120]{0:T(1024)S(1)}, f32[5120]{0:T(1024)}, u32[]{:S(2)}) copy-start(f32[5120]{0:T(1024)} %param.10) | copy-start | bytes 61444
  17.6 10.1 %all-to-all-start = ((bf16[4,32,1280]{2,1,0:T(8,128)(2,1)}), bf16[4,32,1280]{2,1,0:T(8,128)(2,1)S(1)}, u32[]{:S(2)}, u32[]{:S(2)}) async-start(bf16[4,32,1280]{2,1,0:T(8,128)(2,1)} %bitcast.260), calls=%async_computation | async-start | bytes 655360 | tf_op jit(solution)/shard_map/all_to_all | solution.py:54
  21.1 27.2 %all-gather.9.cloned.1.call-start = ((), (), s32[]{:S(2)}) async-start(), calls=%async_computation.7 | async-start | bytes 1638400 | tf_op jit(solution)/shard_map/all_gather | solution.py:66
  29.0 69.5 %all-gather.11.cloned.1.call-start = ((), (), s32[]{:S(2)}) async-start(), calls=%async_computation.8 | async-start | bytes 1179648 | tf_op jit(solution)/shard_map/all_gather | solution.py:76
  29.1 11.1 %copy-start.6 = (bf16[5120,256]{1,0:T(8,128)(2,1)S(1)}, bf16[5120,256]{1,0:T(8,128)(2,1)}, u32[]{:S(2)}) copy-start(bf16[5120,256]{1,0:T(8,128)(2,1)} %param.13) | copy-start | bytes 7864324
  58.1 87.3 %reduce-scatter.5.cloned.1.call-start = ((), (), s32[]{:S(2)}) async-start(), calls=%async_computation.9 | async-start | bytes 3276800 | tf_op jit(solution)/shard_map/reduce_scatter | solution.py:103
  100.6 7.0 slice-start
  102.8 4.8 slice-start.1
  108.6 38.1 %copy-start.8 = (f32[5120]{0:T(1024)S(1)}, f32[5120]{0:T(1024)}, u32[]{:S(2)}) copy-start(f32[5120]{0:T(1024)} %param.11) | copy-start | bytes 61444
  112.0 55.0 %all-gather.13.cloned.1.call-start = ((), (), s32[]{:S(2)}) async-start(), calls=%async_computation.10 | async-start | bytes 1638400 | tf_op jit(solution)/shard_map/all_gather | solution.py:66
  147.0 119.7 %copy-start = (f32[1,32,5120]{2,1,0:T(8,128)}, f32[1,32,5120]{2,1,0:T(8,128)S(1)}, u32[]{:S(2)}) copy-start(f32[1,32,5120]{2,1,0:T(8,128)S(1)} %get-tuple-element.30) | copy-start | bytes 1966084
  148.7 68.6 %all-gather.15.cloned.1.call-start = ((), (), s32[]{:S(2)}) async-start(), calls=%async_computation.11 | async-start | bytes 1179648 | tf_op jit(solution)/shard_map/all_gather | solution.py:76
  176.9 87.3 %reduce-scatter.7.cloned.1.call-start = ((), (), s32[]{:S(2)}) async-start(), calls=%async_computation.12 | async-start | bytes 3276800 | tf_op jit(solution)/shard_map/reduce_scatter | solution.py:103
  219.4 7.0 slice-start.4
  230.8 115.8 %all-gather.17.cloned.1.call-start = ((), (), s32[]{:S(2)}) async-start(), calls=%async_computation.13 | async-start | bytes 1638400 | tf_op jit(solution)/shard_map/all_gather | solution.py:66
  327.5 69.4 %all-gather.19.cloned.1.call-start = ((), (), s32[]{:S(2)}) async-start(), calls=%async_computation.14 | async-start | bytes 1179648 | tf_op jit(solution)/shard_map/all_gather | solution.py:76
  356.5 86.5 %reduce-scatter.9.cloned.1.call-start = ((), (), s32[]{:S(2)}) async-start(), calls=%async_computation.15 | async-start | bytes 3276800 | tf_op jit(solution)/shard_map/reduce_scatter | solution.py:103
  396.9 8.0 %slice-start.8 = ((s8[13107200]{0:T(1024)(128)(4,1)}), s8[524288]{0:T(1024)(128)(4,1)S(1)}, s32[]{:S(2)}) async-start(s8[13107200]{0:T(1024)(128)(4,1)} %bitcast.230), calls=%async_computation.27 | async-start | bytes 1048576
  409.6 126.4 %all-gather.21.cloned.1.call-start = ((), (), s32[]{:S(2)}) async-start(), calls=%async_computation.16 | async-start | bytes 1638400 | tf_op jit(solution)/shard_map/all_gather | solution.py:66
  517.0 69.4 %all-gather.23.cloned.1.call-start = ((), (), s32[]{:S(2)}) async-start(), calls=%async_computation.17 | async-start | bytes 1179648 | tf_op jit(solution)/shard_map/all_gather | solution.py:76
  545.9 87.3 %reduce-scatter.11.cloned.1.call-start = ((), (), s32[]{:S(2)}) async-start(), calls=%async_computation.18 | async-start | bytes 3276800 | tf_op jit(solution)/shard_map/reduce_scatter | solution.py:103
  586.3 9.1 %slice-start.12 = ((s8[13107200]{0:T(1024)(128)(4,1)}), s8[524288]{0:T(1024)(128)(4,1)S(1)}, s32[]{:S(2)}) async-start(s8[13107200]{0:T(1024)(128)(4,1)} %bitcast.232), calls=%async_computation.31 | async-start | bytes 1048576
  590.6 4.8 slice-start.13
  599.8 37.0 %copy-start.1 = (f32[1,32,5120]{2,1,0:T(8,128)S(1)}, f32[1,32,5120]{2,1,0:T(8,128)}, u32[]{:S(2)}) copy-start(f32[1,32,5120]{2,1,0:T(8,128)} %copy-done) | copy-start | bytes 1966084
  (19 other events, 48.2 us)
Sparse Core Ops, SparseCore 0:
  29.1 19.0 all-gather.8
  58.3 40.2 all-gather.10
  112.1 33.2 reduce-scatter.4
  148.9 18.1 all-gather.12
  177.0 40.2 all-gather.14
  230.9 33.2 reduce-scatter.6
  327.6 18.9 all-gather.16
  356.6 40.2 all-gather.18
  409.7 33.2 reduce-scatter.8
  517.1 18.9 all-gather.20
  546.0 40.2 all-gather.22
  600.0 33.2 reduce-scatter.10
